TPU v7x, 512 devices: a whole 4x8x8 slice. The times are simulated.
512 devices in a mesh: chan: 64 (over z, y_hi, core), wall: 8 (over x, y_lo).
Axes of the slice: x: 4, y: 8 (y_hi: 4, y_lo: 2; y = y_hi * 2 + y_lo), z: 8, core: 2. Of those that a mesh axis runs over, the one named last changes fastest.
Arguments:
- coords: float32 [3, 64, 8, 4096], P(None, 'chan', 'wall'), as said below
- masses: float32 [64, 8, 4096], P('chan', 'wall'), may hold values from 0.5 to 2
- counts: int32 [64, 8, 16], P('chan', 'wall'), may hold values from 64 to 256
- lists: int32 [64, 8, 5, 16, 2], P('chan', 'wall'), may hold values from 0 to 47, as said below
Outputs:
- density: float32 [64, 8, 4096], P('chan', 'wall')
Inputs may be any that keep to these rules, and one draw needn't show every extreme that they name: `lists`: each row of 2 entries names different tiles; tile t of extended slab s is s * 16 + t, slab 0 the lower cross-wall neighbour, 1 the slab itself, 2 the upper neighbour. `coords`: channel components lie in [0, 1), cross-wall and depth components in [0, 8).
All inputs are finite; a program needn't handle non-finite values.
Results may differ from a plain program's by a relative error of at most 0.0003.
Values sent between devices are 32-bit elements; how exact they have to be, the bound alone decides.
A program may use at most 64 MiB of HBM per device.

v0:
```python
import math

import jax
import jax.numpy as jnp
from jax import lax
from jax.sharding import PartitionSpec as P

NB = 2
R = 4


def extended_2(block, sides, width):
    for axis, dim in sides:
        count = lax.axis_size(axis)
        forward = [(i, i + 1) for i in range(count - 1)]
        backward = [(target, source) for source, target in forward]
        low = lax.ppermute(
            lax.slice_in_dim(block, block.shape[dim] - width, None, axis=dim), axis, forward
        )
        high = lax.ppermute(lax.slice_in_dim(block, 0, width, axis=dim), axis, backward)
        block = jnp.concatenate([low, block, high], axis=dim)
    return block


def from_behind(block, axis, distance):
    devices = range(lax.axis_size(axis))
    route = [((i - distance) % len(devices), i) for i in devices]
    return lax.ppermute(block, axis, route)


def from_behind_2(block, axis, distance):
    devices = range(lax.axis_size(axis))
    route = [(i - distance, i) for i in devices if i - distance in devices]
    return lax.ppermute(block, axis, route)


def spline(scaled):
    return (jnp.maximum(2.0 - scaled, 0.0) ** 3 * 0.25 - jnp.maximum(1.0 - scaled, 0.0) ** 3) * (
        1.0 / math.pi
    )


def pair_block(own_block, partner, partner_rows, offset, with_back):
    tile_count = own_block.shape[1]
    tile_len = own_block.shape[2]
    list_len = partner_rows.shape[1]
    picked = jnp.take(partner, partner_rows.reshape(-1), axis=1).reshape(
        4, tile_count, list_len, tile_len
    )
    wall_lift = (partner_rows // tile_count - 1).astype(jnp.float32) * (2.0 * R)
    reach = float(R)

    def single_tile(inputs):
        own_tile, theirs, shift_y = inputs
        delta_x = own_tile[0][None, :, None] - (theirs[0][:, None, :] + offset)
        delta_y = own_tile[1][None, :, None] - (theirs[1][:, None, :] + shift_y[:, None, None])
        delta_z = own_tile[2][None, :, None] - theirs[2][:, None, :]
        distance = jnp.sqrt(delta_x * delta_x + delta_y * delta_y + delta_z * delta_z + 0.0001)
        weight = spline(distance / reach)
        gained = jnp.sum(weight * theirs[3][:, None, :], axis=(0, 2))
        handed = jnp.sum(weight * own_tile[3][None, :, None], axis=1)
        return (gained, handed)

    group = math.gcd(tile_count, 4)

    def grouped(values):
        return values.reshape((tile_count // group, group) + values.shape[1:])

    gained, handed = lax.map(
        jax.vmap(single_tile),
        (
            grouped(jnp.moveaxis(own_block, 1, 0)),
            grouped(jnp.moveaxis(picked, 1, 0)),
            grouped(wall_lift),
        ),
    )
    gained = gained.reshape(tile_count, tile_len)
    handed = handed.reshape(tile_count, list_len, tile_len)
    if not with_back:
        return (gained, None)
    onehot = (
        partner_rows.reshape(-1)[:, None] == jnp.arange(partner.shape[1], dtype=jnp.int32)[None, :]
    ).astype(jnp.float32)
    returned = jnp.dot(onehot.T, handed.reshape(-1, tile_len), precision=lax.Precision.HIGHEST)
    return (gained, returned)


def on_device(coords, masses, counts, lists):
    tile_count = counts.shape[2]
    tile_len = masses.shape[2] // tile_count
    slots = jnp.arange(tile_len, dtype=jnp.int32)
    filled = (slots[None, :] < counts[0, 0][:, None]).astype(jnp.float32)
    weighted = masses.reshape(tile_count, tile_len) * filled
    packed = jnp.concatenate([coords, weighted.reshape(1, 1, 1, -1)], axis=0)
    extended = extended_2(packed, (("wall", 2),), 1)
    extended = extended.reshape(4, 3 * tile_count, tile_len)
    own_block = packed.reshape(4, tile_count, tile_len)
    partner_rows = lists[0, 0]
    density, unused_back = pair_block(own_block, extended, partner_rows[0], 0.0, False)
    returns = jnp.zeros((3 * tile_count, tile_len), jnp.float32)
    for step in range(1, R + 1):
        partner = from_behind(extended, "chan", -step)
        gained, handed = pair_block(own_block, partner, partner_rows[step], float(step), True)
        density = density + gained
        returns = returns + from_behind(handed, "chan", step)
    from_below = from_behind_2(returns[2 * tile_count :], "wall", 1)
    from_above = from_behind_2(returns[:tile_count], "wall", -1)
    total = density + returns[tile_count : 2 * tile_count] + from_below + from_above
    return (total * filled / (NB * tile_len)).reshape(1, 1, -1)


def solution(mesh):
    placed = (
        P(None, "chan", "wall", None),
        P("chan", "wall", None),
        P("chan", "wall", None),
        P("chan", "wall", None, None, None),
    )
    return jax.shard_map(
        on_device, mesh=mesh, in_specs=placed, out_specs=P("chan", "wall", None), check_vma=False
    )
```

profile of v0, /device:TPU:204, one launch (start us, length us, event | category | flops | bytes accessed | tf_op | source)
XLA Modules:
  0.0 140.6 jit_solution(3880399559653819791)
XLA Ops:
  0.0 0.8 iota_compare_fusion.4
  0.8 0.7 bitcast_select_fusion
  1.6 0.9 pad_maximum_fusion.2
  2.4 3.0 %collective-permute-start = (f32[4,1,1,4096]{3,2,1,0:T(1,128)S(1)}, f32[4,1,1,4096]{3,2,1,0:T(1,128)S(1)}, u32[]{:S(2)}, u32[]{:S(2)}) collective-permute-start(f32[4,1,1,4096]{3,2,1,0:T(1,128)S(1)} %pad_maximum_fusion.2), channel_id=1, source_target_pairs={{0,1},{1,2},{2,3},{3,4},{4,5},{5,6},{6,7},{8,9},{9,10},{10,11},{11... | collective-permute-start | bytes 196616 | tf_op jit(solution)/shard_map/ppermute | solution.py:17
  5.4 2.9 %collective-permute-start.1 = (f32[4,1,1,4096]{3,2,1,0:T(1,128)S(1)}, f32[4,1,1,4096]{3,2,1,0:T(1,128)S(1)}, u32[]{:S(2)}, u32[]{:S(2)}) collective-permute-start(f32[4,1,1,4096]{3,2,1,0:T(1,128)S(1)} %pad_maximum_fusion.2), channel_id=1, source_target_pairs={{1,0},{2,1},{3,2},{4,3},{5,4},{6,5},{7,6},{9,8},{10,9},{11,10},{12... | collective-permute-start | bytes 196616 | tf_op jit(solution)/shard_map/ppermute | solution.py:20
  8.3 0.8 fusion.68
  10.6 0.1 reduce
  10.9 1.6 %collective-permute-done.1 = f32[4,1,1,4096]{3,2,1,0:T(1,128)S(1)} collective-permute-done((f32[4,1,1,4096]{3,2,1,0:T(1,128)S(1)}, f32[4,1,1,4096]{3,2,1,0:T(1,128)S(1)}, u32[]{:S(2)}, u32[]{:S(2)}) %collective-permute-start.1) | collective-permute-done | bytes 65568 | tf_op jit(solution)/shard_map/ppermute | solution.py:20
  12.5 0.2 pad_maximum_fusion
  12.7 0.1 reshape.315
  12.8 0.1 copy.104
  13.0 4.8 %collective-permute-start.4 = (f32[4,48,256]{2,0,1:T(4,128)S(1)}, f32[4,48,256]{2,0,1:T(4,128)S(1)}, u32[]{:S(2)}, u32[]{:S(2)}) collective-permute-start(f32[4,48,256]{2,0,1:T(4,128)S(1)} %copy.104), channel_id=1, source_target_pairs={{24,0},{32,8},{40,16},{48,24},{56,32},{64,40},{72,48},{80,56},{88,... | collective-permute-start | bytes 589832 | tf_op jit(solution)/shard_map/ppermute | solution.py:28
  17.8 2.3 %collective-permute-start.3 = (f32[4,48,256]{2,0,1:T(4,128)S(1)}, f32[4,48,256]{2,0,1:T(4,128)S(1)}, u32[]{:S(2)}, u32[]{:S(2)}) collective-permute-start(f32[4,48,256]{2,0,1:T(4,128)S(1)} %copy.104), channel_id=1, source_target_pairs={{16,0},{24,8},{32,16},{40,24},{48,32},{56,40},{64,48},{72,56},{80,... | collective-permute-start | bytes 589832 | tf_op jit(solution)/shard_map/ppermute | solution.py:28
  20.2 3.8 %collective-permute-start.2 = (f32[4,48,256]{2,0,1:T(4,128)S(1)}, f32[4,48,256]{2,0,1:T(4,128)S(1)}, u32[]{:S(2)}, u32[]{:S(2)}) collective-permute-start(f32[4,48,256]{2,0,1:T(4,128)S(1)} %copy.104), channel_id=1, source_target_pairs={{8,0},{16,8},{24,16},{32,24},{40,32},{48,40},{56,48},{64,56},{72,6... | collective-permute-start | bytes 589832 | tf_op jit(solution)/shard_map/ppermute | solution.py:28
  24.0 5.0 %collective-permute-start.5 = (f32[4,48,256]{2,0,1:T(4,128)S(1)}, f32[4,48,256]{2,0,1:T(4,128)S(1)}, u32[]{:S(2)}, u32[]{:S(2)}) collective-permute-start(f32[4,48,256]{2,0,1:T(4,128)S(1)} %copy.104), channel_id=1, source_target_pairs={{32,0},{40,8},{48,16},{56,24},{64,32},{72,40},{80,48},{88,56},{96,... | collective-permute-start | bytes 589832 | tf_op jit(solution)/shard_map/ppermute | solution.py:28
  29.0 0.6 gather_fusion
  29.6 0.1 broadcast_select_fusion.4
  29.8 0.6 gather_fusion.3
  30.4 0.1 broadcast_select_fusion.1
  30.5 12.6 %while.61 = (s32[]{:T(128)}, f32[4,4,256]{2,1,0:T(4,128)S(1)}, f32[4,4,2,256]{3,2,1,0:T(2,128)S(1)}, f32[4,4,4,256]{3,1,2,0:T(4,128)S(1)}, f32[4,4,4,2,256]{4,2,...) while((s32[]{:T(128)}, f32[4,4,256]{2,1,0:T(4,128)S(1)}, f32[4,4,2,256]{3,2,1,0:T(2,128)S(1)}, ...), condition=%wide.region_14.16_spmd, body=%wide.region_11.15_spmd.sunk | while | flops 12587010 | bytes 348417 | solution.py:69
  30.6 0.1 copy.165
  30.8 2.8 %multiply_reduce_fusion.14 = (f32[4,2,256]{2,1,0:T(2,128)S(1)}, f32[4,256]{1,0:T(4,128)S(1)}) fusion(f32[4,256]{1,0:T(4,128)S(1)} %get-tuple-element.665, f32[4,2,256]{2,1,0:T(2,128)S(1)} %get-tuple-element.666, f32[4,256]{1,0:T(4,128)S(1)} %get-tuple-element.667, f32[4,2,256]{2,1,0:T(2,128)S(1)} %fusion.90, f32[4,256]{1,0:T(4,128)S(1)} %get-tuple-element.668, ...), kind=kLoop, calls=%fused_computation.77.clone.1 | loop fusion | flops 12579840 | bytes 61440 | tf_op jit(solution)/shard_map/while/body/eval_jaxpr/vmap()/reduce_sum | solution.py:61
  33.8 0.1 copy.165
  34.0 2.8 %multiply_reduce_fusion.14 = (f32[4,2,256]{2,1,0:T(2,128)S(1)}, f32[4,256]{1,0:T(4,128)S(1)}) fusion(f32[4,256]{1,0:T(4,128)S(1)} %get-tuple-element.665, f32[4,2,256]{2,1,0:T(2,128)S(1)} %get-tuple-element.666, f32[4,256]{1,0:T(4,128)S(1)} %get-tuple-element.667, f32[4,2,256]{2,1,0:T(2,128)S(1)} %fusion.90, f32[4,256]{1,0:T(4,128)S(1)} %get-tuple-element.668, ...), kind=kLoop, calls=%fused_computation.77.clone.1 | loop fusion | flops 12579840 | bytes 61440 | tf_op jit(solution)/shard_map/while/body/eval_jaxpr/vmap()/reduce_sum | solution.py:61
  37.1 2.8 %multiply_reduce_fusion.14 = (f32[4,2,256]{2,1,0:T(2,128)S(1)}, f32[4,256]{1,0:T(4,128)S(1)}) fusion(f32[4,256]{1,0:T(4,128)S(1)} %get-tuple-element.665, f32[4,2,256]{2,1,0:T(2,128)S(1)} %get-tuple-element.666, f32[4,256]{1,0:T(4,128)S(1)} %get-tuple-element.667, f32[4,2,256]{2,1,0:T(2,128)S(1)} %fusion.90, f32[4,256]{1,0:T(4,128)S(1)} %get-tuple-element.668, ...), kind=kLoop, calls=%fused_computation.77.clone.1 | loop fusion | flops 12579840 | bytes 61440 | tf_op jit(solution)/shard_map/while/body/eval_jaxpr/vmap()/reduce_sum | solution.py:61
  40.2 2.8 %multiply_reduce_fusion.14 = (f32[4,2,256]{2,1,0:T(2,128)S(1)}, f32[4,256]{1,0:T(4,128)S(1)}) fusion(f32[4,256]{1,0:T(4,128)S(1)} %get-tuple-element.665, f32[4,2,256]{2,1,0:T(2,128)S(1)} %get-tuple-element.666, f32[4,256]{1,0:T(4,128)S(1)} %get-tuple-element.667, f32[4,2,256]{2,1,0:T(2,128)S(1)} %fusion.90, f32[4,256]{1,0:T(4,128)S(1)} %get-tuple-element.668, ...), kind=kLoop, calls=%fused_computation.77.clone.1 | loop fusion | flops 12579840 | bytes 61440 | tf_op jit(solution)/shard_map/while/body/eval_jaxpr/vmap()/reduce_sum | solution.py:61
  43.1 0.6 gather_fusion.2
  43.8 0.1 broadcast_select_fusion.2
  43.9 12.6 %while.60 = (s32[]{:T(128)}, f32[4,4,256]{2,1,0:T(4,128)S(1)}, f32[4,4,2,256]{3,2,1,0:T(2,128)S(1)}, f32[4,4,4,256]{3,1,2,0:T(4,128)S(1)}, f32[4,4,4,2,256]{4,2,...) while((s32[]{:T(128)}, f32[4,4,256]{2,1,0:T(4,128)S(1)}, f32[4,4,2,256]{3,2,1,0:T(2,128)S(1)}, ...), condition=%wide.region_10.12_spmd, body=%wide.region_7.11_spmd.sunk | while | flops 12587010 | bytes 348417 | solution.py:69
  44.2 2.8 %multiply_reduce_fusion.13 = (f32[4,2,256]{2,1,0:T(2,128)S(1)}, f32[4,256]{1,0:T(4,128)S(1)}) fusion(f32[4,256]{1,0:T(4,128)S(1)} %get-tuple-element.650, f32[4,2,256]{2,1,0:T(2,128)S(1)} %get-tuple-element.651, f32[4,256]{1,0:T(4,128)S(1)} %get-tuple-element.652, f32[4,2,256]{2,1,0:T(2,128)S(1)} %fusion.88, f32[4,256]{1,0:T(4,128)S(1)} %get-tuple-element.653, ...), kind=kLoop, calls=%fused_computation.53.clone.1 | loop fusion | flops 12579840 | bytes 61440 | tf_op jit(solution)/shard_map/while/body/eval_jaxpr/vmap()/reduce_sum | solution.py:61
  47.3 2.8 %multiply_reduce_fusion.13 = (f32[4,2,256]{2,1,0:T(2,128)S(1)}, f32[4,256]{1,0:T(4,128)S(1)}) fusion(f32[4,256]{1,0:T(4,128)S(1)} %get-tuple-element.650, f32[4,2,256]{2,1,0:T(2,128)S(1)} %get-tuple-element.651, f32[4,256]{1,0:T(4,128)S(1)} %get-tuple-element.652, f32[4,2,256]{2,1,0:T(2,128)S(1)} %fusion.88, f32[4,256]{1,0:T(4,128)S(1)} %get-tuple-element.653, ...), kind=kLoop, calls=%fused_computation.53.clone.1 | loop fusion | flops 12579840 | bytes 61440 | tf_op jit(solution)/shard_map/while/body/eval_jaxpr/vmap()/reduce_sum | solution.py:61
  50.5 2.8 %multiply_reduce_fusion.13 = (f32[4,2,256]{2,1,0:T(2,128)S(1)}, f32[4,256]{1,0:T(4,128)S(1)}) fusion(f32[4,256]{1,0:T(4,128)S(1)} %get-tuple-element.650, f32[4,2,256]{2,1,0:T(2,128)S(1)} %get-tuple-element.651, f32[4,256]{1,0:T(4,128)S(1)} %get-tuple-element.652, f32[4,2,256]{2,1,0:T(2,128)S(1)} %fusion.88, f32[4,256]{1,0:T(4,128)S(1)} %get-tuple-element.653, ...), kind=kLoop, calls=%fused_computation.53.clone.1 | loop fusion | flops 12579840 | bytes 61440 | tf_op jit(solution)/shard_map/while/body/eval_jaxpr/vmap()/reduce_sum | solution.py:61
  53.6 2.8 %multiply_reduce_fusion.13 = (f32[4,2,256]{2,1,0:T(2,128)S(1)}, f32[4,256]{1,0:T(4,128)S(1)}) fusion(f32[4,256]{1,0:T(4,128)S(1)} %get-tuple-element.650, f32[4,2,256]{2,1,0:T(2,128)S(1)} %get-tuple-element.651, f32[4,256]{1,0:T(4,128)S(1)} %get-tuple-element.652, f32[4,2,256]{2,1,0:T(2,128)S(1)} %fusion.88, f32[4,256]{1,0:T(4,128)S(1)} %get-tuple-element.653, ...), kind=kLoop, calls=%fused_computation.53.clone.1 | loop fusion | flops 12579840 | bytes 61440 | tf_op jit(solution)/shard_map/while/body/eval_jaxpr/vmap()/reduce_sum | solution.py:61
  56.5 0.6 gather_fusion.1
  57.1 0.1 broadcast_select_fusion.3
  57.2 12.6 %while.59 = (s32[]{:T(128)}, f32[4,4,256]{2,1,0:T(4,128)S(1)}, f32[4,4,2,256]{3,2,1,0:T(2,128)S(1)}, f32[4,4,4,256]{3,1,2,0:T(4,128)S(1)}, f32[4,4,4,2,256]{4,2,...) while((s32[]{:T(128)}, f32[4,4,256]{2,1,0:T(4,128)S(1)}, f32[4,4,2,256]{3,2,1,0:T(2,128)S(1)}, ...), condition=%wide.region_6.8_spmd, body=%wide.region_3.7_spmd.sunk | while | flops 12587010 | bytes 348417 | solution.py:69
  57.5 2.8 %multiply_reduce_fusion.12 = (f32[4,2,256]{2,1,0:T(2,128)S(1)}, f32[4,256]{1,0:T(4,128)S(1)}) fusion(f32[4,256]{1,0:T(4,128)S(1)} %get-tuple-element.635, f32[4,2,256]{2,1,0:T(2,128)S(1)} %get-tuple-element.636, f32[4,256]{1,0:T(4,128)S(1)} %get-tuple-element.637, f32[4,2,256]{2,1,0:T(2,128)S(1)} %fusion.86, f32[4,256]{1,0:T(4,128)S(1)} %get-tuple-element.638, ...), kind=kLoop, calls=%fused_computation.29.clone.1 | loop fusion | flops 12579840 | bytes 61440 | tf_op jit(solution)/shard_map/while/body/eval_jaxpr/vmap()/reduce_sum | solution.py:61
  60.7 2.8 %multiply_reduce_fusion.12 = (f32[4,2,256]{2,1,0:T(2,128)S(1)}, f32[4,256]{1,0:T(4,128)S(1)}) fusion(f32[4,256]{1,0:T(4,128)S(1)} %get-tuple-element.635, f32[4,2,256]{2,1,0:T(2,128)S(1)} %get-tuple-element.636, f32[4,256]{1,0:T(4,128)S(1)} %get-tuple-element.637, f32[4,2,256]{2,1,0:T(2,128)S(1)} %fusion.86, f32[4,256]{1,0:T(4,128)S(1)} %get-tuple-element.638, ...), kind=kLoop, calls=%fused_computation.29.clone.1 | loop fusion | flops 12579840 | bytes 61440 | tf_op jit(solution)/shard_map/while/body/eval_jaxpr/vmap()/reduce_sum | solution.py:61
  63.8 2.8 %multiply_reduce_fusion.12 = (f32[4,2,256]{2,1,0:T(2,128)S(1)}, f32[4,256]{1,0:T(4,128)S(1)}) fusion(f32[4,256]{1,0:T(4,128)S(1)} %get-tuple-element.635, f32[4,2,256]{2,1,0:T(2,128)S(1)} %get-tuple-element.636, f32[4,256]{1,0:T(4,128)S(1)} %get-tuple-element.637, f32[4,2,256]{2,1,0:T(2,128)S(1)} %fusion.86, f32[4,256]{1,0:T(4,128)S(1)} %get-tuple-element.638, ...), kind=kLoop, calls=%fused_computation.29.clone.1 | loop fusion | flops 12579840 | bytes 61440 | tf_op jit(solution)/shard_map/while/body/eval_jaxpr/vmap()/reduce_sum | solution.py:61
  66.9 2.8 %multiply_reduce_fusion.12 = (f32[4,2,256]{2,1,0:T(2,128)S(1)}, f32[4,256]{1,0:T(4,128)S(1)}) fusion(f32[4,256]{1,0:T(4,128)S(1)} %get-tuple-element.635, f32[4,2,256]{2,1,0:T(2,128)S(1)} %get-tuple-element.636, f32[4,256]{1,0:T(4,128)S(1)} %get-tuple-element.637, f32[4,2,256]{2,1,0:T(2,128)S(1)} %fusion.86, f32[4,256]{1,0:T(4,128)S(1)} %get-tuple-element.638, ...), kind=kLoop, calls=%fused_computation.29.clone.1 | loop fusion | flops 12579840 | bytes 61440 | tf_op jit(solution)/shard_map/while/body/eval_jaxpr/vmap()/reduce_sum | solution.py:61
  69.8 0.6 gather_fusion.4
  70.5 0.1 broadcast_select_fusion
  70.6 12.6 %while.62 = (s32[]{:T(128)}, f32[4,4,256]{2,1,0:T(4,128)S(1)}, f32[4,4,2,256]{3,2,1,0:T(2,128)S(1)}, f32[4,4,4,256]{3,1,2,0:T(4,128)S(1)}, f32[4,4,4,2,256]{4,2,...) while((s32[]{:T(128)}, f32[4,4,256]{2,1,0:T(4,128)S(1)}, f32[4,4,2,256]{3,2,1,0:T(2,128)S(1)}, ...), condition=%wide.region_18.20_spmd, body=%wide.region_15.19_spmd.sunk | while | flops 12587010 | bytes 348417 | solution.py:69
  70.9 2.8 %multiply_reduce_fusion.15 = (f32[4,2,256]{2,1,0:T(2,128)S(1)}, f32[4,256]{1,0:T(4,128)S(1)}) fusion(f32[4,256]{1,0:T(4,128)S(1)} %get-tuple-element.680, f32[4,2,256]{2,1,0:T(2,128)S(1)} %get-tuple-element.681, f32[4,256]{1,0:T(4,128)S(1)} %get-tuple-element.682, f32[4,2,256]{2,1,0:T(2,128)S(1)} %fusion.92, f32[4,256]{1,0:T(4,128)S(1)} %get-tuple-element.683, ...), kind=kLoop, calls=%fused_computation.101.clone.1 | loop fusion | flops 12579840 | bytes 61440 | tf_op jit(solution)/shard_map/while/body/eval_jaxpr/vmap()/reduce_sum | solution.py:61
  74.0 2.8 %multiply_reduce_fusion.15 = (f32[4,2,256]{2,1,0:T(2,128)S(1)}, f32[4,256]{1,0:T(4,128)S(1)}) fusion(f32[4,256]{1,0:T(4,128)S(1)} %get-tuple-element.680, f32[4,2,256]{2,1,0:T(2,128)S(1)} %get-tuple-element.681, f32[4,256]{1,0:T(4,128)S(1)} %get-tuple-element.682, f32[4,2,256]{2,1,0:T(2,128)S(1)} %fusion.92, f32[4,256]{1,0:T(4,128)S(1)} %get-tuple-element.683, ...), kind=kLoop, calls=%fused_computation.101.clone.1 | loop fusion | flops 12579840 | bytes 61440 | tf_op jit(solution)/shard_map/while/body/eval_jaxpr/vmap()/reduce_sum | solution.py:61
  77.2 2.8 %multiply_reduce_fusion.15 = (f32[4,2,256]{2,1,0:T(2,128)S(1)}, f32[4,256]{1,0:T(4,128)S(1)}) fusion(f32[4,256]{1,0:T(4,128)S(1)} %get-tuple-element.680, f32[4,2,256]{2,1,0:T(2,128)S(1)} %get-tuple-element.681, f32[4,256]{1,0:T(4,128)S(1)} %get-tuple-element.682, f32[4,2,256]{2,1,0:T(2,128)S(1)} %fusion.92, f32[4,256]{1,0:T(4,128)S(1)} %get-tuple-element.683, ...), kind=kLoop, calls=%fused_computation.101.clone.1 | loop fusion | flops 12579840 | bytes 61440 | tf_op jit(solution)/shard_map/while/body/eval_jaxpr/vmap()/reduce_sum | solution.py:61
  80.3 2.8 %multiply_reduce_fusion.15 = (f32[4,2,256]{2,1,0:T(2,128)S(1)}, f32[4,256]{1,0:T(4,128)S(1)}) fusion(f32[4,256]{1,0:T(4,128)S(1)} %get-tuple-element.680, f32[4,2,256]{2,1,0:T(2,128)S(1)} %get-tuple-element.681, f32[4,256]{1,0:T(4,128)S(1)} %get-tuple-element.682, f32[4,2,256]{2,1,0:T(2,128)S(1)} %fusion.92, f32[4,256]{1,0:T(4,128)S(1)} %get-tuple-element.683, ...), kind=kLoop, calls=%fused_computation.101.clone.1 | loop fusion | flops 12579840 | bytes 61440 | tf_op jit(solution)/shard_map/while/body/eval_jaxpr/vmap()/reduce_sum | solution.py:61
  83.2 0.3 fusion.34
  83.5 6.7 %collective-permute-start.6 = (f32[48,256]{1,0:T(8,128)S(1)}, f32[48,256]{1,0:T(8,128)S(1)}, u32[]{:S(2)}, u32[]{:S(2)}) collective-permute-start(f32[48,256]{1,0:T(8,128)S(1)} %fusion.34), channel_id=1, source_target_pairs={{504,0},{0,8},{8,16},{16,24},{24,32},{32,40},{40,48},{48,56},{56,6... | collective-permute-start | bytes 147464 | tf_op jit(solution)/shard_map/ppermute | solution.py:28
  90.2 0.3 fusion.35
  90.5 1.9 %collective-permute-start.7 = (f32[48,256]{1,0:T(8,128)S(1)}, f32[48,256]{1,0:T(8,128)S(1)}, u32[]{:S(2)}, u32[]{:S(2)}) collective-permute-start(f32[48,256]{1,0:T(8,128)S(1)} %fusion.35), channel_id=1, source_target_pairs={{496,0},{504,8},{0,16},{8,24},{16,32},{24,40},{32,48},{40,56},{48,... | collective-permute-start | bytes 147464 | tf_op jit(solution)/shard_map/ppermute | solution.py:28
  92.5 0.3 fusion.36
  92.8 6.9 %collective-permute-start.8 = (f32[48,256]{1,0:T(8,128)S(1)}, f32[48,256]{1,0:T(8,128)S(1)}, u32[]{:S(2)}, u32[]{:S(2)}) collective-permute-start(f32[48,256]{1,0:T(8,128)S(1)} %fusion.36), channel_id=1, source_target_pairs={{488,0},{496,8},{504,16},{0,24},{8,32},{16,40},{24,48},{32,56},{40... | collective-permute-start | bytes 147464 | tf_op jit(solution)/shard_map/ppermute | solution.py:28
  99.7 0.3 fusion.37
  100.0 5.8 %collective-permute-start.9 = (f32[48,256]{1,0:T(8,128)S(1)}, f32[48,256]{1,0:T(8,128)S(1)}, u32[]{:S(2)}, u32[]{:S(2)}) collective-permute-start(f32[48,256]{1,0:T(8,128)S(1)} %fusion.37), channel_id=1, source_target_pairs={{480,0},{488,8},{496,16},{504,24},{0,32},{8,40},{16,48},{24,56},{3... | collective-permute-start | bytes 147464 | tf_op jit(solution)/shard_map/ppermute | solution.py:28
  105.8 12.4 %while.58 = (s32[]{:T(128)}, f32[4,4,256]{2,1,0:T(4,128)S(1)}, f32[4,4,4,256]{3,1,2,0:T(4,128)S(1)}, f32[4,4,4,2,256]{4,2,3,1,0:T(4,128)S(1)}, f32[4,4,2]{1,0,2:T(4,128)S(1)}, /*index=5*/s32[]{:T(128)}) while((s32[]{:T(128)}, f32[4,4,256]{2,1,0:T(4,128)S(1)}, f32[4,4,4,256]{3,1,2,0:T(4,128)S(1)}, f32[4,4,4,2,256]{4,2,3,1,0:T(4,128)S(1)}, ...), condition=%wide.region_2.4_spmd, body=%wide.region_0.3_spmd.sunk | while | flops 11537410 | bytes 311541 | solution.py:69
  106.1 2.8 %fusion.84 = f32[4,256]{1,0:T(4,128)S(1)} fusion(f32[4,2,256]{2,1,0:T(2,128)S(1)} %get-tuple-element.623, f32[4,2,256]{2,1,0:T(2,128)S(1)} %get-tuple-element.624, f32[4,256]{1,0:T(4,128)S(1)} %get-tuple-element.625, f32[4,2,256]{2,1,0:T(2,128)S(1)} %fusion.83, f32[4,256]{1,0:T(4,128)S(1)} %get-tuple-element.626, ...), kind=kLoop, calls=%fused_computation.10.clone.1 | loop fusion | flops 11533312 | bytes 49152 | tf_op jit(solution)/shard_map/while/body/eval_jaxpr/vmap()/reduce_sum | solution.py:60
  109.2 2.8 %fusion.84 = f32[4,256]{1,0:T(4,128)S(1)} fusion(f32[4,2,256]{2,1,0:T(2,128)S(1)} %get-tuple-element.623, f32[4,2,256]{2,1,0:T(2,128)S(1)} %get-tuple-element.624, f32[4,256]{1,0:T(4,128)S(1)} %get-tuple-element.625, f32[4,2,256]{2,1,0:T(2,128)S(1)} %fusion.83, f32[4,256]{1,0:T(4,128)S(1)} %get-tuple-element.626, ...), kind=kLoop, calls=%fused_computation.10.clone.1 | loop fusion | flops 11533312 | bytes 49152 | tf_op jit(solution)/shard_map/while/body/eval_jaxpr/vmap()/reduce_sum | solution.py:60
  112.3 2.8 %fusion.84 = f32[4,256]{1,0:T(4,128)S(1)} fusion(f32[4,2,256]{2,1,0:T(2,128)S(1)} %get-tuple-element.623, f32[4,2,256]{2,1,0:T(2,128)S(1)} %get-tuple-element.624, f32[4,256]{1,0:T(4,128)S(1)} %get-tuple-element.625, f32[4,2,256]{2,1,0:T(2,128)S(1)} %fusion.83, f32[4,256]{1,0:T(4,128)S(1)} %get-tuple-element.626, ...), kind=kLoop, calls=%fused_computation.10.clone.1 | loop fusion | flops 11533312 | bytes 49152 | tf_op jit(solution)/shard_map/while/body/eval_jaxpr/vmap()/reduce_sum | solution.py:60
  115.4 2.8 %fusion.84 = f32[4,256]{1,0:T(4,128)S(1)} fusion(f32[4,2,256]{2,1,0:T(2,128)S(1)} %get-tuple-element.623, f32[4,2,256]{2,1,0:T(2,128)S(1)} %get-tuple-element.624, f32[4,256]{1,0:T(4,128)S(1)} %get-tuple-element.625, f32[4,2,256]{2,1,0:T(2,128)S(1)} %fusion.83, f32[4,256]{1,0:T(4,128)S(1)} %get-tuple-element.626, ...), kind=kLoop, calls=%fused_computation.10.clone.1 | loop fusion | flops 11533312 | bytes 49152 | tf_op jit(solution)/shard_map/while/body/eval_jaxpr/vmap()/reduce_sum | solution.py:60
  118.3 15.1 %collective-permute-start.10 = (f32[16,256]{1,0:T(8,128)S(1)}, f32[16,256]{1,0:T(8,128)S(1)}, u32[]{:S(2)}, u32[]{:S(2)}) collective-permute-start(f32[16,256]{1,0:T(8,128)S(1)} %get-tuple-element.419), channel_id=1, source_target_pairs={{0,1},{1,2},{2,3},{3,4},{4,5},{5,6},{6,7},{8,9},{9,10},{10,11},{11... | collective-permute-start | bytes 49160 | tf_op jit(solution)/shard_map/ppermute | solution.py:34
  133.4 1.9 %collective-permute-start.11 = (f32[16,256]{1,0:T(8,128)S(1)}, f32[16,256]{1,0:T(8,128)S(1)}, u32[]{:S(2)}, u32[]{:S(2)}) collective-permute-start(f32[16,256]{1,0:T(8,128)S(1)} %get-tuple-element.420), channel_id=1, source_target_pairs={{1,0},{2,1},{3,2},{4,3},{5,4},{6,5},{7,6},{9,8},{10,9},{11,10},{12... | collective-permute-start | bytes 49160 | tf_op jit(solution)/shard_map/ppermute | solution.py:34
  135.3 4.6 %collective-permute-done.11 = f32[16,256]{1,0:T(8,128)S(1)} collective-permute-done((f32[16,256]{1,0:T(8,128)S(1)}, f32[16,256]{1,0:T(8,128)S(1)}, u32[]{:S(2)}, u32[]{:S(2)}) %collective-permute-start.11) | collective-permute-done | bytes 16416 | tf_op jit(solution)/shard_map/ppermute | solution.py:34
  140.0 0.6 reshape.326
  (267 shorter events, 6.8 us)
Async XLA Ops:
  0.0 10.5 %copy-start.2 = (s32[1,1,16]{2,1,0:T(1,128)S(1)}, s32[1,1,16]{2,1,0:T(1,128)}, u32[]{:S(2)}) copy-start(s32[1,1,16]{2,1,0:T(1,128)} %param.18) | copy-start | bytes 196
  0.0 10.5 %copy-start.1 = (f32[1,1,4096]{2,1,0:T(1,128)S(1)}, f32[1,1,4096]{2,1,0:T(1,128)}, u32[]{:S(2)}) copy-start(f32[1,1,4096]{2,1,0:T(1,128)} %param.17) | copy-start | bytes 49156
  0.0 10.6 %copy-start = (f32[3,1,1,4096]{3,2,1,0:T(1,128)S(1)}, f32[3,1,1,4096]{3,2,1,0:T(1,128)}, u32[]{:S(2)}) copy-start(f32[3,1,1,4096]{3,2,1,0:T(1,128)} %param.16) | copy-start | bytes 147460
  2.4 8.5 %collective-permute-start = (f32[4,1,1,4096]{3,2,1,0:T(1,128)S(1)}, f32[4,1,1,4096]{3,2,1,0:T(1,128)S(1)}, u32[]{:S(2)}, u32[]{:S(2)}) collective-permute-start(f32[4,1,1,4096]{3,2,1,0:T(1,128)S(1)} %pad_maximum_fusion.2), channel_id=1, source_target_pairs={{0,1},{1,2},{2,3},{3,4},{4,5},{5,6},{6,7},{8,9},{9,10},{10,11},{11... | collective-permute-start | bytes 196616 | tf_op jit(solution)/shard_map/ppermute | solution.py:17
  5.4 7.1 %collective-permute-start.1 = (f32[4,1,1,4096]{3,2,1,0:T(1,128)S(1)}, f32[4,1,1,4096]{3,2,1,0:T(1,128)S(1)}, u32[]{:S(2)}, u32[]{:S(2)}) collective-permute-start(f32[4,1,1,4096]{3,2,1,0:T(1,128)S(1)} %pad_maximum_fusion.2), channel_id=1, source_target_pairs={{1,0},{2,1},{3,2},{4,3},{5,4},{6,5},{7,6},{9,8},{10,9},{11,10},{12... | collective-permute-start | bytes 196616 | tf_op jit(solution)/shard_map/ppermute | solution.py:20
  13.0 16.8 %collective-permute-start.4 = (f32[4,48,256]{2,0,1:T(4,128)S(1)}, f32[4,48,256]{2,0,1:T(4,128)S(1)}, u32[]{:S(2)}, u32[]{:S(2)}) collective-permute-start(f32[4,48,256]{2,0,1:T(4,128)S(1)} %copy.104), channel_id=1, source_target_pairs={{24,0},{32,8},{40,16},{48,24},{56,32},{64,40},{72,48},{80,56},{88,... | collective-permute-start | bytes 589832 | tf_op jit(solution)/shard_map/ppermute | solution.py:28
  17.8 25.3 %collective-permute-start.3 = (f32[4,48,256]{2,0,1:T(4,128)S(1)}, f32[4,48,256]{2,0,1:T(4,128)S(1)}, u32[]{:S(2)}, u32[]{:S(2)}) collective-permute-start(f32[4,48,256]{2,0,1:T(4,128)S(1)} %copy.104), channel_id=1, source_target_pairs={{16,0},{24,8},{32,16},{40,24},{48,32},{56,40},{64,48},{72,56},{80,... | collective-permute-start | bytes 589832 | tf_op jit(solution)/shard_map/ppermute | solution.py:28
  20.2 36.3 %collective-permute-start.2 = (f32[4,48,256]{2,0,1:T(4,128)S(1)}, f32[4,48,256]{2,0,1:T(4,128)S(1)}, u32[]{:S(2)}, u32[]{:S(2)}) collective-permute-start(f32[4,48,256]{2,0,1:T(4,128)S(1)} %copy.104), channel_id=1, source_target_pairs={{8,0},{16,8},{24,16},{32,24},{40,32},{48,40},{56,48},{64,56},{72,6... | collective-permute-start | bytes 589832 | tf_op jit(solution)/shard_map/ppermute | solution.py:28
  24.0 45.8 %collective-permute-start.5 = (f32[4,48,256]{2,0,1:T(4,128)S(1)}, f32[4,48,256]{2,0,1:T(4,128)S(1)}, u32[]{:S(2)}, u32[]{:S(2)}) collective-permute-start(f32[4,48,256]{2,0,1:T(4,128)S(1)} %copy.104), channel_id=1, source_target_pairs={{32,0},{40,8},{48,16},{56,24},{64,32},{72,40},{80,48},{88,56},{96,... | collective-permute-start | bytes 589832 | tf_op jit(solution)/shard_map/ppermute | solution.py:28
  83.5 34.8 %collective-permute-start.6 = (f32[48,256]{1,0:T(8,128)S(1)}, f32[48,256]{1,0:T(8,128)S(1)}, u32[]{:S(2)}, u32[]{:S(2)}) collective-permute-start(f32[48,256]{1,0:T(8,128)S(1)} %fusion.34), channel_id=1, source_target_pairs={{504,0},{0,8},{8,16},{16,24},{24,32},{32,40},{40,48},{48,56},{56,6... | collective-permute-start | bytes 147464 | tf_op jit(solution)/shard_map/ppermute | solution.py:28
  90.5 27.7 %collective-permute-start.7 = (f32[48,256]{1,0:T(8,128)S(1)}, f32[48,256]{1,0:T(8,128)S(1)}, u32[]{:S(2)}, u32[]{:S(2)}) collective-permute-start(f32[48,256]{1,0:T(8,128)S(1)} %fusion.35), channel_id=1, source_target_pairs={{496,0},{504,8},{0,16},{8,24},{16,32},{24,40},{32,48},{40,56},{48,... | collective-permute-start | bytes 147464 | tf_op jit(solution)/shard_map/ppermute | solution.py:28
  92.8 25.5 %collective-permute-start.8 = (f32[48,256]{1,0:T(8,128)S(1)}, f32[48,256]{1,0:T(8,128)S(1)}, u32[]{:S(2)}, u32[]{:S(2)}) collective-permute-start(f32[48,256]{1,0:T(8,128)S(1)} %fusion.36), channel_id=1, source_target_pairs={{488,0},{496,8},{504,16},{0,24},{8,32},{16,40},{24,48},{32,56},{40... | collective-permute-start | bytes 147464 | tf_op jit(solution)/shard_map/ppermute | solution.py:28
  100.0 18.3 %collective-permute-start.9 = (f32[48,256]{1,0:T(8,128)S(1)}, f32[48,256]{1,0:T(8,128)S(1)}, u32[]{:S(2)}, u32[]{:S(2)}) collective-permute-start(f32[48,256]{1,0:T(8,128)S(1)} %fusion.37), channel_id=1, source_target_pairs={{480,0},{488,8},{496,16},{504,24},{0,32},{8,40},{16,48},{24,56},{3... | collective-permute-start | bytes 147464 | tf_op jit(solution)/shard_map/ppermute | solution.py:28
  118.3 17.0 %collective-permute-start.10 = (f32[16,256]{1,0:T(8,128)S(1)}, f32[16,256]{1,0:T(8,128)S(1)}, u32[]{:S(2)}, u32[]{:S(2)}) collective-permute-start(f32[16,256]{1,0:T(8,128)S(1)} %get-tuple-element.419), channel_id=1, source_target_pairs={{0,1},{1,2},{2,3},{3,4},{4,5},{5,6},{6,7},{8,9},{9,10},{10,11},{11... | collective-permute-start | bytes 49160 | tf_op jit(solution)/shard_map/ppermute | solution.py:34
  133.4 6.5 %collective-permute-start.11 = (f32[16,256]{1,0:T(8,128)S(1)}, f32[16,256]{1,0:T(8,128)S(1)}, u32[]{:S(2)}, u32[]{:S(2)}) collective-permute-start(f32[16,256]{1,0:T(8,128)S(1)} %get-tuple-element.420), channel_id=1, source_target_pairs={{1,0},{2,1},{3,2},{4,3},{5,4},{6,5},{7,6},{9,8},{10,9},{11,10},{12... | collective-permute-start | bytes 49160 | tf_op jit(solution)/shard_map/ppermute | solution.py:34
where the time goes:
time: 141 us
  other arithmetic  61.6 us (44%)
  starting transfers between devices  60.1 us (43%)
  local copies, waits for them, and re-layouts  9.61 us (7%)
  waiting for transfers between devices  6.15 us (4%)
    reduce_sum x16, other arithmetic, single_tile(): handed = jnp.sum(weight * own_tile[3][None, :, None], axis=1)  45 us
    ppermute x8, starting transfers between devices, from_behind(): return lax.ppermute(block, axis, route)  37.3 us
    ppermute x2, starting transfers between devices, from_behind_2(): return lax.ppermute(block, axis, route)  17 us
    reduce_sum x4, other arithmetic, single_tile(): gained = jnp.sum(weight * theirs[3][:, None, :], axis=(0, 2))  11.2 us
    ppermute x2, waiting for transfers between devices, from_behind_2(): return lax.ppermute(block, axis, route)  4.56 us
    gather x5, local copies, waits for them, and re-layouts, pair_block(): jnp.take(partner, partner_rows.reshape(-1), axis=1)  3.16 us
    ppermute x1, starting transfers between devices, extended_2(): lax.ppermute(lax.slice_in_dim(block, block.shape[dim] - width, None, axis...  2.99 us
    ppermute x1, starting transfers between devices, extended_2(): lax.ppermute(lax.slice_in_dim(block, 0, width, axis=dim), axis, backward)  2.85 us
  transfers between devices with their start and end apart: 12, of which 2 were waited for; matrix products, arithmetic and copies ran while one was open for 39% of the time, Pallas kernels for 0%

commit v1 on v0

v1 whole, which is shorter than its diff:
```python
import functools
import math

import jax
import jax.numpy as jnp
from jax import lax
from jax.experimental import pallas as pl
from jax.experimental.pallas import tpu as pltpu
from jax.sharding import PartitionSpec as P

R = 4
TILES = 16
TILE = 256
ROWS = 32
EPS = 0.0001 / (R * R)
CHUNK = 32
F32 = jnp.float32
BF16 = jnp.bfloat16
MESH = pl.DeviceIdType.MESH


def split3(value):
    high = value.astype(BF16).astype(F32)
    rest = value - high
    mid = rest.astype(BF16).astype(F32)
    low = (rest - mid).astype(BF16).astype(F32)
    return high, mid, low


def rows_a(value):
    h, m, l = split3(value)
    return [h, h, m, m, h, l]


def rows_b(value):
    h, m, l = split3(value)
    return [h, m, h, m, l, h]


def features_a(x, y, z, w):
    one = jnp.ones_like(x)
    norm = x * x + y * y + z * z + EPS
    rows = rows_a(-2.0 * x) + rows_a(-2.0 * y) + rows_a(-2.0 * z)
    rows += list(split3(norm)) + [one] * 3 + rows_a(w)
    return rows + [jnp.zeros_like(x)] * 2


def features_b(x, y, z, w):
    one = jnp.ones_like(x)
    norm = x * x + y * y + z * z
    rows = rows_b(x) + rows_b(y) + rows_b(z)
    rows += [one] * 3 + list(split3(norm)) + rows_b(w)
    return rows + [jnp.zeros_like(x)] * 2


def kernel(
    chan_count,
    wall_count,
    coords_ref,
    mass_ref,
    counts_ref,
    lists_ref,
    out_ref,
    own,
    walls,
    slabs,
    list_v,
    list_s,
    stage,
    feat_b,
    feat_a,
    dots0,
    dots1,
    part_g,
    full_g,
    gained,
    gained_in,
    handed_rows,
    list_row,
    handed,
    handed_in,
    slab_send,
    slab_recv,
    wall_send,
    wall_recv,
    list_send,
    list_recv,
    gain_send,
    gain_recv,
    hand_send,
    hand_recv,
    list_copy,
):
    c = lax.axis_index("chan")
    w = lax.axis_index("wall")
    has_low = w > 0
    has_high = w < wall_count - 1

    def up(k):
        return (lax.rem(c + k, chan_count), w)

    def down(k):
        return (lax.rem(c + chan_count - k, chan_count), w)

    barrier = pltpu.get_barrier_semaphore()
    for k in range(1, R + 1):
        pl.semaphore_signal(barrier, inc=1, device_id=up(k), device_id_type=MESH)
        pl.semaphore_signal(barrier, inc=1, device_id=down(k), device_id_type=MESH)

    @pl.when(has_low)
    def _():
        pl.semaphore_signal(barrier, inc=1, device_id=(c, w - 1), device_id_type=MESH)

    @pl.when(has_high)
    def _():
        pl.semaphore_signal(barrier, inc=1, device_id=(c, w + 1), device_id_type=MESH)

    row_at = lax.broadcasted_iota(jnp.int32, (ROWS, 128), 0)
    lane_at = lax.broadcasted_iota(jnp.int32, (ROWS, 128), 1)
    slot_at = lax.rem(row_at, 2) * 128 + lane_at
    limit = jnp.zeros((ROWS, 128), jnp.int32)
    for t in range(TILES):
        limit = jnp.where(row_at // 2 == t, counts_ref[t], limit)
    filled = (slot_at < limit).astype(F32)
    own[0:32, :] = coords_ref[0:32, :] * (1.0 / R)
    own[32:64, :] = (coords_ref[32:64, :] - R) * (1.0 / R)
    own[64:96, :] = (coords_ref[64:96, :] - R) * (1.0 / R)
    own[96:128, :] = mass_ref[...] * filled
    full_g[...] = jnp.zeros_like(full_g)
    list_row[...] = jnp.zeros_like(list_row)

    pl.semaphore_wait(barrier, 2 * R + has_low.astype(jnp.int32) + has_high.astype(jnp.int32))

    def wall_copy(slot, target):
        return pltpu.make_async_remote_copy(
            src_ref=own,
            dst_ref=walls.at[slot],
            send_sem=wall_send.at[slot],
            recv_sem=wall_recv.at[slot],
            device_id=(c, target),
            device_id_type=MESH,
        )

    def slab_copy(k):
        return pltpu.make_async_remote_copy(
            src_ref=own,
            dst_ref=slabs.at[k - 1],
            send_sem=slab_send.at[k - 1],
            recv_sem=slab_recv.at[k - 1],
            device_id=up(k),
            device_id_type=MESH,
        )

    def list_send_copy(k):
        return pltpu.make_async_remote_copy(
            src_ref=lists_ref.at[k],
            dst_ref=list_v.at[k],
            send_sem=list_send.at[k - 1],
            recv_sem=list_recv.at[k - 1],
            device_id=up(k),
            device_id_type=MESH,
        )

    def gain_copy(k):
        return pltpu.make_async_remote_copy(
            src_ref=gained.at[k, pl.ds(8, ROWS)],
            dst_ref=gained_in.at[k - 1],
            send_sem=gain_send.at[k - 1],
            recv_sem=gain_recv.at[k - 1],
            device_id=down(k),
            device_id_type=MESH,
        )

    def hand_copy(slot, target):
        return pltpu.make_async_remote_copy(
            src_ref=handed.at[pl.ds(64 * (1 - slot), ROWS)],
            dst_ref=handed_in.at[slot],
            send_sem=hand_send.at[slot],
            recv_sem=hand_recv.at[slot],
            device_id=(c, target),
            device_id_type=MESH,
        )

    @pl.when(has_high)
    def _():
        wall_copy(0, w + 1).start()

    @pl.when(has_low)
    def _():
        wall_copy(1, w - 1).start()

    for k in range(1, R + 1):
        list_send_copy(k).start()
        slab_copy(k).start()

    def stage_rows(rows):
        for f, row in enumerate(rows):
            stage[f * ROWS : (f + 1) * ROWS, :] = row

    feature_at = lax.broadcasted_iota(jnp.int32, (ROWS, 128), 0)

    def build_b(read, side):
        stage_rows(features_b(read(0), read(1) + 2.0 * (side - 1), read(2), read(3)))

        def one(t, carry):
            for half in range(2):
                block = stage[pl.ds(2 * t + half, ROWS, stride=ROWS), :]
                squared = jnp.where(feature_at < 24, block, 0.0).astype(BF16)
                weights = jnp.where(feature_at < 24, 0.0, block).astype(BF16)
                feat_b[side * TILES + t, :, half * 128 : half * 128 + 128] = squared
                feat_b[side * TILES + t, :, 256 + half * 128 : 384 + half * 128] = weights
            return carry

        lax.fori_loop(0, TILES, one, 0)

    def build_a(read, k):
        shift = jnp.asarray(k, jnp.int32).astype(F32) * (1.0 / R)
        stage_rows(features_a(read(0) - shift, read(1), read(2), read(3)))

        def one(t, carry):
            for half in range(2):
                block = stage[pl.ds(2 * t + half, ROWS, stride=ROWS), :]
                feat_a[pl.ds(pl.multiple_of(t * TILE + half * 128, 128), 128), :] = block.T.astype(BF16)
            return carry

        lax.fori_loop(0, TILES, one, 0)

    def own_rows(i):
        return own[32 * i : 32 * i + 32, :]

    build_b(own_rows, 1)

    @pl.when(has_low)
    def _():
        wall_copy(0, w).wait_recv()

    @pl.when(jnp.logical_not(has_low))
    def _():
        walls[0] = jnp.zeros_like(walls[0])

    build_b(lambda i: walls[0, 32 * i : 32 * i + 32, :], 0)

    @pl.when(has_high)
    def _():
        wall_copy(1, w).wait_recv()

    @pl.when(jnp.logical_not(has_high))
    def _():
        walls[1] = jnp.zeros_like(walls[1])

    build_b(lambda i: walls[1, 32 * i : 32 * i + 32, :], 2)

    lane_row = lax.broadcasted_iota(jnp.int32, (1, 128), 1)

    def pair(dots, source, target):
        taken = jnp.zeros((8, TILE), F32)
        for r in range(0, TILE, CHUNK):
            square = dots[r : r + CHUNK, 0:TILE]
            mass = dots[r : r + CHUNK, TILE : 2 * TILE]
            near = 2.0 - square * lax.rsqrt(square)
            outer = near * near * near
            inner = 4.0 - 3.0 * (square * near)
            value = jnp.maximum(jnp.minimum(inner, outer), 0.0) * mass
            row = value[:, 0:128] + value[:, 128:256]
            if source is not None:
                row = row + source[r : r + CHUNK, :]
            target[r : r + CHUNK, :] = row
            for e in range(0, CHUNK, 8):
                taken = taken + value[e : e + 8, :]
        return jnp.sum(taken, axis=0, keepdims=True)

    def section(k, with_back):
        def dot_into(dots, i, n):
            tile = feat_a[pl.ds(pl.multiple_of(i * TILE, TILE), TILE), :]
            j = list_s[k, n, i]
            dots[...] = jnp.dot(tile, feat_b[j], preferred_element_type=F32)

        def flush(i):
            summed = jnp.sum(full_g[...].T, axis=0, keepdims=True)
            gained[k, pl.ds(2 * i + 6, 1), :] = summed[:, 0:128]
            gained[k, pl.ds(2 * i + 7, 1), :] = summed[:, 128:256]

        def note(i, n, row):
            if with_back:
                at = (k - 1) * 32 + 2 * i + n
                handed_rows[pl.ds(at, 1), :] = row
                list_row[...] = jnp.where(lane_row == at, list_s[k, n, i], list_row[...])

        def body(i, carry):
            dot_into(dots1, i, 1)
            flush(i)
            note(i, 0, pair(dots0, None, part_g))
            dot_into(dots0, jnp.minimum(i + 1, TILES - 1), 0)
            note(i, 1, pair(dots1, part_g, full_g))
            return carry

        dot_into(dots0, 0, 0)
        lax.fori_loop(0, TILES, body, 0)
        flush(TILES)

    def far(k, carry):
        list_send_copy(k).wait_recv()
        copy = pltpu.make_async_copy(list_v.at[k], list_s.at[k], list_copy)
        copy.start()
        slab_copy(k).wait_recv()
        build_a(lambda i: slabs[k - 1, 32 * i : 32 * i + 32, :], k)
        copy.wait()
        section(k, True)
        gain_copy(k).start()
        return carry

    lax.fori_loop(1, R + 1, far, 0)

    hot = (lax.broadcasted_iota(jnp.int32, (48, 128), 0) == list_row[...]).astype(F32).astype(BF16)
    summed = jnp.zeros((48, TILE), F32)
    for piece in split3(handed_rows[...]):
        summed = summed + jnp.dot(hot, piece.astype(BF16), preferred_element_type=F32)
    handed[pl.ds(0, 48, stride=2), :] = summed[:, 0:128]
    handed[pl.ds(1, 48, stride=2), :] = summed[:, 128:256]

    copy = pltpu.make_async_copy(lists_ref.at[0], list_s.at[0], list_copy)
    copy.start()
    build_a(own_rows, 0)
    copy.wait()

    @pl.when(has_high)
    def _():
        hand_copy(0, w + 1).start()

    @pl.when(has_low)
    def _():
        hand_copy(1, w - 1).start()

    section(0, False)

    total = gained[0, 8:40, :] + handed[32:64, :]
    for k in range(1, R + 1):
        gain_copy(k).wait_recv()
        total = total + gained_in[k - 1]
    out_ref[...] = total

    @pl.when(has_low)
    def _():
        hand_copy(0, w).wait_recv()
        out_ref[...] += handed_in[0]

    @pl.when(has_high)
    def _():
        hand_copy(1, w).wait_recv()
        out_ref[...] += handed_in[1]

    scale = filled * (1.0 / (4.0 * math.pi * 2 * TILE))
    out_ref[...] = out_ref[...] * scale / mass_ref[...]

    for k in range(1, R + 1):
        slab_copy(k).wait_send()
        list_send_copy(k).wait_send()
        gain_copy(k).wait_send()

    @pl.when(has_high)
    def _():
        wall_copy(0, w).wait_send()
        hand_copy(0, w).wait_send()

    @pl.when(has_low)
    def _():
        wall_copy(1, w).wait_send()
        hand_copy(1, w).wait_send()


def solution(mesh):
    placed = (
        P(None, "chan", "wall", None),
        P("chan", "wall", None),
        P("chan", "wall", None),
        P("chan", "wall", None, None, None),
    )
    chan_count = mesh.shape["chan"]
    wall_count = mesh.shape["wall"]

    def on_device(coords, masses, counts, lists):
        vmem = pl.BlockSpec(memory_space=pltpu.VMEM)
        smem = pl.BlockSpec(memory_space=pltpu.SMEM)
        dma = pltpu.SemaphoreType.DMA
        density = pl.pallas_call(
            functools.partial(kernel, chan_count, wall_count),
            out_shape=jax.ShapeDtypeStruct((ROWS, 128), F32),
            in_specs=[vmem, vmem, smem, vmem],
            out_specs=vmem,
            scratch_shapes=[
                pltpu.VMEM((128, 128), F32),
                pltpu.VMEM((2, 128, 128), F32),
                pltpu.VMEM((R, 128, 128), F32),
                pltpu.VMEM((R + 1, 2, 16), jnp.int32),
                pltpu.SMEM((R + 1, 2, 16), jnp.int32),
                pltpu.VMEM((32 * ROWS, 128), F32),
                pltpu.VMEM((48, 32, 512), BF16),
                pltpu.VMEM((TILES * TILE, 32), BF16),
                pltpu.VMEM((TILE, 512), F32),
                pltpu.VMEM((TILE, 512), F32),
                pltpu.VMEM((TILE, 128), F32),
                pltpu.VMEM((TILE, 128), F32),
                pltpu.VMEM((R + 1, 40, 128), F32),
                pltpu.VMEM((R, ROWS, 128), F32),
                pltpu.VMEM((128, TILE), F32),
                pltpu.VMEM((1, 128), jnp.int32),
                pltpu.VMEM((96, 128), F32),
                pltpu.VMEM((2, ROWS, 128), F32),
                dma((R,)),
                dma((R,)),
                dma((2,)),
                dma((2,)),
                dma((R,)),
                dma((R,)),
                dma((R,)),
                dma((R,)),
                dma((2,)),
                dma((2,)),
                dma(()),
            ],
            compiler_params=pltpu.CompilerParams(collective_id=0, has_side_effects=True),
        )(
            coords.reshape(3 * ROWS, 128),
            masses.reshape(ROWS, 128),
            counts.reshape(TILES),
            jnp.transpose(lists.reshape(R + 1, TILES, 2), (0, 2, 1)),
        )
        return density.reshape(1, 1, -1)

    return jax.shard_map(
        on_device, mesh=mesh, in_specs=placed, out_specs=P("chan", "wall", None), check_vma=False
    )
```

time: 141 us -> 67.2 us (0.48)
  the two profiles are of different devices: /device:TPU:204 before, /device:TPU:4 now
where the time goes in v1:
time: 67.2 us; the launch traced here: 67 us
  Pallas kernels  65.7 us (98%)
  local copies, waits for them, and re-layouts  1.32 us (2%)
    pallas_call x1, Pallas kernels, on_device(): pl.pallas_call(functools.partial(kernel, chan_count, wall_count), out_sha...  65.7 us

profile of v1, /device:TPU:4, one launch (start us, length us, event | category | flops | bytes accessed | tf_op | source)
XLA Modules:
  0.0 67.0 jit_solution(1532869047235047672)
XLA Ops:
  0.0 65.7 %shard_map.46 = f32[32,128]{1,0:T(8,128)} custom-call(f32[96,128]{1,0:T(8,128)} %bitcast.8, f32[32,128]{1,0:T(8,128)} %bitcast.9, s32[16]{0:T(128)} %bitcast.11, s32[5,2,16]{2,1,0:T(2,128)} %bitcast.10), custom_call_target="tpu_custom_call" | custom-call | tf_op jit(solution)/shard_map/pallas_call | solution.py:385
  65.7 1.3 %copy.6 = f32[1,1,4096]{2,1,0:T(1,128)} copy(f32[1,1,4096]{2,1,0:T(1,128)} %bitcast.7) | data formatting | bytes 32768

commit v2 on v1

v2 whole, which is shorter than its diff:
```python
import functools
import math

import jax
import jax.numpy as jnp
from jax import lax
from jax.experimental import pallas as pl
from jax.experimental.pallas import tpu as pltpu
from jax.sharding import PartitionSpec as P

R = 4
TILES = 16
TILE = 256
ROWS = 32
EPS = 0.0001 / (R * R)
CHUNK = 32
UNROLL = 4
FAR = 16.0
F32 = jnp.float32
BF16 = jnp.bfloat16
MESH = pl.DeviceIdType.MESH


def split3(value):
    high = value.astype(BF16).astype(F32)
    rest = value - high
    mid = rest.astype(BF16).astype(F32)
    low = (rest - mid).astype(BF16).astype(F32)
    return high, mid, low


def spread4(value, row):
    swapped = jnp.where(row % 2 == 0, pltpu.roll(value, 7, 1), pltpu.roll(value, 1, 1))
    value = value + swapped
    swapped = jnp.where(row % 4 < 2, pltpu.roll(value, 6, 1), pltpu.roll(value, 2, 1))
    return value + swapped


def halves(first, upper, lower, row):
    upper_turned, lower_turned = pltpu.roll(upper, 4, 1), pltpu.roll(lower, 4, 1)
    top = row < 4
    if first == 0:
        return jnp.where(top, upper, lower_turned)
    return jnp.where(top, upper_turned, lower)


def rows_of(value):
    return lax.broadcasted_iota(jnp.int32, value.shape, 1)


def features_a(packed, shift):
    row = rows_of(packed)
    moved = packed - jnp.where(row % 4 == 0, shift, 0.0)
    coord = row % 4 < 3
    norm = spread4(jnp.where(coord, moved * moved, 0.0), row) + EPS
    high, mid, low = split3(jnp.where(coord, -2.0 * moved, norm))
    mass = split3(spread4(jnp.where(coord, 0.0, packed), row))
    blocks = []
    for half in range(2):
        wide = [halves(half, part, part, row) for part in mass]
        last = jnp.where(row == 3, wide[0], jnp.where(row == 4, wide[1], wide[2]))
        last = jnp.where(row < 3, 1.0, jnp.where(row < 6, last, 0.0))
        blocks.append(
            [
                halves(half, high, high, row),
                halves(half, mid, mid, row),
                halves(half, high, low, row),
                last,
            ]
        )
    return blocks


def features_b(packed, lift):
    row = rows_of(packed)
    coord = row % 4 < 3
    mass = spread4(jnp.where(coord, 0.0, packed), row)
    empty = mass <= 0.0
    mass = jnp.where(empty, 1.0, mass)
    root = jnp.exp(jnp.log(mass) * (1.0 / 3.0))
    root = root - (root * root * root - mass) / (3.0 * root * root)
    square = root * root
    moved = packed + jnp.where(row % 4 == 1, lift, 0.0)
    moved = jnp.where(jnp.logical_and(row % 4 == 2, empty), FAR, moved)
    norm = spread4(jnp.where(coord, moved * moved, 0.0), row) * square
    moved = jnp.where(coord, moved, 1.0) * square
    blocks = []
    parts = []
    for factor in (1.0, 3.0):
        parts.append((split3(factor * moved), split3(factor * norm)))
    for half in range(2):
        block = []
        for (high, mid, low), last in parts:
            last = jnp.where(row % 4 == 0, last[0], jnp.where(row % 4 == 1, last[1], last[2]))
            last = jnp.where(row < 3, halves(half, last, last, row), 0.0)
            mixed = halves(half, high, mid, row)
            block.append([mixed, mixed, halves(half, low, high, row), last])
        block.append(halves(half, 2.0 * root, 2.0 * root, row))
        block.append(halves(half, 4.0 * mass, 4.0 * mass, row))
        blocks.append(block)
    return blocks


def kernel(
    chan_count,
    wall_count,
    coords_ref,
    mass_ref,
    counts_ref,
    lists_ref,
    out_ref,
    walls,
    slabs,
    list_v,
    list_s,
    stage,
    feat_b,
    root_b,
    feat_a,
    dots0,
    dots1,
    mass0,
    mass1,
    part_g,
    full_g,
    gained,
    gained_in,
    handed_rows,
    list_row,
    handed,
    handed_in,
    slab_send,
    slab_recv,
    wall_send,
    wall_recv,
    list_send,
    list_recv,
    gain_send,
    gain_recv,
    hand_send,
    hand_recv,
    list_copy,
):
    c = lax.axis_index("chan")
    w = lax.axis_index("wall")
    has_low = w > 0
    has_high = w < wall_count - 1

    def up(k):
        return (lax.rem(c + k, chan_count), w)

    def down(k):
        return (lax.rem(c + chan_count - k, chan_count), w)

    barrier = pltpu.get_barrier_semaphore()
    for k in range(1, R + 1):
        pl.semaphore_signal(barrier, inc=1, device_id=up(k), device_id_type=MESH)
        pl.semaphore_signal(barrier, inc=1, device_id=down(k), device_id_type=MESH)

    @pl.when(has_low)
    def _():
        pl.semaphore_signal(barrier, inc=1, device_id=(c, w - 1), device_id_type=MESH)

    @pl.when(has_high)
    def _():
        pl.semaphore_signal(barrier, inc=1, device_id=(c, w + 1), device_id_type=MESH)

    row_at = lax.broadcasted_iota(jnp.int32, (ROWS, 128), 0)
    lane_at = lax.broadcasted_iota(jnp.int32, (ROWS, 128), 1)
    slot_at = lax.rem(row_at, 2) * 128 + lane_at
    limit = jnp.zeros((ROWS, 128), jnp.int32)
    for t in range(TILES):
        limit = jnp.where(row_at // 2 == t, counts_ref[t], limit)
    filled = (slot_at < limit).astype(F32)
    own = slabs.at[R]
    own[pl.ds(0, ROWS, stride=4), :] = coords_ref[0:32, :] * (1.0 / R)
    own[pl.ds(1, ROWS, stride=4), :] = (coords_ref[32:64, :] - R) * (1.0 / R)
    own[pl.ds(2, ROWS, stride=4), :] = (coords_ref[64:96, :] - R) * (1.0 / R)
    own[pl.ds(3, ROWS, stride=4), :] = mass_ref[...] * filled
    full_g[...] = jnp.zeros_like(full_g)
    list_row[...] = jnp.zeros_like(list_row)

    pl.semaphore_wait(barrier, 2 * R + has_low.astype(jnp.int32) + has_high.astype(jnp.int32))

    def wall_copy(slot, target):
        return pltpu.make_async_remote_copy(
            src_ref=own,
            dst_ref=walls.at[slot],
            send_sem=wall_send.at[slot],
            recv_sem=wall_recv.at[slot],
            device_id=(c, target),
            device_id_type=MESH,
        )

    def slab_copy(k):
        return pltpu.make_async_remote_copy(
            src_ref=own,
            dst_ref=slabs.at[k - 1],
            send_sem=slab_send.at[k - 1],
            recv_sem=slab_recv.at[k - 1],
            device_id=up(k),
            device_id_type=MESH,
        )

    def list_send_copy(k):
        return pltpu.make_async_remote_copy(
            src_ref=lists_ref.at[k],
            dst_ref=list_v.at[k],
            send_sem=list_send.at[k - 1],
            recv_sem=list_recv.at[k - 1],
            device_id=up(k),
            device_id_type=MESH,
        )

    def gain_copy(k):
        return pltpu.make_async_remote_copy(
            src_ref=gained.at[k, pl.ds(8, ROWS)],
            dst_ref=gained_in.at[k - 1],
            send_sem=gain_send.at[k - 1],
            recv_sem=gain_recv.at[k - 1],
            device_id=down(k),
            device_id_type=MESH,
        )

    def hand_copy(slot, target):
        return pltpu.make_async_remote_copy(
            src_ref=handed.at[pl.ds(64 * (1 - slot), ROWS)],
            dst_ref=handed_in.at[slot],
            send_sem=hand_send.at[slot],
            recv_sem=hand_recv.at[slot],
            device_id=(c, target),
            device_id_type=MESH,
        )

    @pl.when(has_high)
    def _():
        wall_copy(0, w + 1).start()

    @pl.when(has_low)
    def _():
        wall_copy(1, w - 1).start()

    for k in range(1, R + 1):
        list_send_copy(k).start()
        slab_copy(k).start()

    def list_down(k):
        source = list_v.at[k]
        return pltpu.make_async_copy(source, list_s.at[k], list_copy.at[k])

    def own_list_down():
        return pltpu.make_async_copy(lists_ref.at[0], list_s.at[0], list_copy.at[0])

    own_list_down().start()

    def build_b(packed, side):
        blocks = features_b(packed.reshape(TILES, 8, 128), 2.0 * (side - 1))
        tiles = slice(side * TILES, side * TILES + TILES)
        for half, (plain, triple, root, mass) in enumerate(blocks):
            lanes = slice(half * 128, half * 128 + 128)
            for at, rows in ((0, plain), (256, triple)):
                wide = slice(at + half * 128, at + half * 128 + 128)
                for g in range(0, 4, 2):
                    both = jnp.concatenate(rows[g : g + 2], axis=1).astype(BF16)
                    feat_b[tiles, 8 * g : 8 * g + 16, wide] = both
            root_b[tiles, 0:8, lanes] = root
            root_b[tiles, 8:16, lanes] = mass

    def build_a(packed, shift):
        blocks = features_a(packed.reshape(TILES, 8, 128), shift)
        for half in range(2):
            for g in range(4):
                stage[half, :, 8 * g : 8 * g + 8, :] = blocks[half][g]

        def some(s, carry):
            for e in range(4):
                t = 4 * s + e
                for half in range(2):
                    spot = pl.multiple_of(t * TILE + half * 128, 128)
                    feat_a[pl.ds(spot, 128), :] = stage[half, t].T.astype(BF16)
            return carry

        lax.fori_loop(0, TILES // 4, some, 0)

    build_b(own[...], 1)

    @pl.when(has_low)
    def _():
        wall_copy(0, w).wait_recv()

    @pl.when(jnp.logical_not(has_low))
    def _():
        walls[0] = jnp.zeros_like(walls[0])

    build_b(walls[0], 0)

    @pl.when(has_high)
    def _():
        wall_copy(1, w).wait_recv()

    @pl.when(jnp.logical_not(has_high))
    def _():
        walls[1] = jnp.zeros_like(walls[1])

    build_b(walls[1], 2)

    lane_row = lax.broadcasted_iota(jnp.int32, (1, 128), 1)
    pick_at = lax.broadcasted_iota(jnp.int32, (32, 128), 0)
    pick = jnp.logical_and(pick_at >= 27, pick_at < 30).astype(F32).astype(BF16)

    def pair(dots, roots, mass, source, target):
        taken = jnp.zeros((8, TILE), F32)
        root = roots[0:8, :][None]
        top = roots[8:16, :][None]
        for r in range(0, TILE, CHUNK):
            square = dots[r : r + CHUNK, 0:TILE].reshape(CHUNK // 8, 8, TILE)
            triple = dots[r : r + CHUNK, TILE : 2 * TILE].reshape(CHUNK // 8, 8, TILE)
            near = root - square * lax.rsqrt(square)
            outer = near * near * near
            inner = top - triple * near
            value = jnp.maximum(jnp.minimum(inner, outer), 0.0)
            low, high = value[:, :, 0:128], value[:, :, 128:256]
            row = (low + high).reshape(CHUNK, 128)
            if source is not None:
                row = row + source[r : r + CHUNK, :]
            target[r : r + CHUNK, :] = row
            weight = mass[r : r + CHUNK, :].reshape(CHUNK // 8, 8, 128)
            back = jnp.concatenate([low * weight, high * weight], axis=2)
            for e in range(CHUNK // 8):
                taken = taken + back[e]
        return jnp.sum(taken, axis=0, keepdims=True)

    def section(step, k):
        def a_tile(i):
            return feat_a[pl.ds(pl.multiple_of(i * TILE, TILE), TILE), :]

        def dot_into(dots, i, n):
            dots[...] = jnp.dot(a_tile(i), feat_b[list_s[k, n, i]], preferred_element_type=F32)

        def mass_into(mass, i):
            mass[...] = jnp.dot(a_tile(i), pick, preferred_element_type=F32)

        def flush(i):
            summed = jnp.sum(full_g[...].T, axis=0, keepdims=True)
            gained[k, pl.ds(2 * i + 6, 1), :] = summed[:, 0:128]
            gained[k, pl.ds(2 * i + 7, 1), :] = summed[:, 128:256]

        def note(i, n, row):
            at = step * 32 + 2 * i + n
            handed_rows[pl.ds(at, 1), :] = row
            list_row[...] = jnp.where(lane_row == at, list_s[k, n, i], list_row[...])

        masses = (mass0, mass1)

        def body(s, carry):
            for u in range(UNROLL):
                i = s * UNROLL + u
                after = jnp.minimum(i + 1, TILES - 1)
                mass = masses[u % 2]
                dot_into(dots1, i, 1)
                flush(i)
                note(i, 0, pair(dots0, root_b.at[list_s[k, 0, i]], mass, None, part_g))
                dot_into(dots0, after, 0)
                mass_into(masses[(u + 1) % 2], after)
                note(i, 1, pair(dots1, root_b.at[list_s[k, 1, i]], mass, part_g, full_g))
            return carry

        dot_into(dots0, 0, 0)
        mass_into(mass0, 0)
        lax.fori_loop(0, TILES // UNROLL, body, 0)
        flush(TILES)

    list_send_copy(1).wait_recv()
    list_down(1).start()

    def one_offset(step, carry):
        k = lax.rem(step + 1, R + 1)

        @pl.when(step < R - 1)
        def _():
            list_send_copy(k + 1).wait_recv()
            list_down(k + 1).start()

        @pl.when(step < R)
        def _():
            slab_copy(k).wait_recv()
            list_down(k).wait()

        build_a(slabs[step], k.astype(F32) * (1.0 / R))

        @pl.when(step == R)
        def _():
            own_list_down().wait()
            known = list_row[...]
            hot = (lax.broadcasted_iota(jnp.int32, (48, 128), 0) == known).astype(F32).astype(BF16)
            summed = jnp.zeros((48, TILE), F32)
            for piece in split3(handed_rows[0:128, :]):
                summed = summed + jnp.dot(hot, piece.astype(BF16), preferred_element_type=F32)
            handed[pl.ds(0, 48, stride=2), :] = summed[:, 0:128]
            handed[pl.ds(1, 48, stride=2), :] = summed[:, 128:256]

        @pl.when(jnp.logical_and(step == R, has_high))
        def _():
            hand_copy(0, w + 1).start()

        @pl.when(jnp.logical_and(step == R, has_low))
        def _():
            hand_copy(1, w - 1).start()

        section(step, k)

        @pl.when(step < R)
        def _():
            gain_copy(k).start()

        return carry

    lax.fori_loop(0, R + 1, one_offset, 0)

    total = gained[0, 8:40, :]
    for k in range(1, R + 1):
        gain_copy(k).wait_recv()
        total = total + gained_in[k - 1]
    out_ref[...] = handed[32:64, :]

    @pl.when(has_low)
    def _():
        hand_copy(0, w).wait_recv()
        out_ref[...] += handed_in[0]

    @pl.when(has_high)
    def _():
        hand_copy(1, w).wait_recv()
        out_ref[...] += handed_in[1]

    scale = filled * (1.0 / (4.0 * math.pi * 2 * TILE))
    out_ref[...] = (total + out_ref[...] / mass_ref[...]) * scale

    for k in range(1, R + 1):
        slab_copy(k).wait_send()
        list_send_copy(k).wait_send()
        gain_copy(k).wait_send()

    @pl.when(has_high)
    def _():
        wall_copy(0, w).wait_send()
        hand_copy(0, w).wait_send()

    @pl.when(has_low)
    def _():
        wall_copy(1, w).wait_send()
        hand_copy(1, w).wait_send()


def solution(mesh):
    placed = (
        P(None, "chan", "wall", None),
        P("chan", "wall", None),
        P("chan", "wall", None),
        P("chan", "wall", None, None, None),
    )
    chan_count = mesh.shape["chan"]
    wall_count = mesh.shape["wall"]

    def on_device(coords, masses, counts, lists):
        vmem = pl.BlockSpec(memory_space=pltpu.VMEM)
        smem = pl.BlockSpec(memory_space=pltpu.SMEM)
        dma = pltpu.SemaphoreType.DMA
        density = pl.pallas_call(
            functools.partial(kernel, chan_count, wall_count),
            out_shape=jax.ShapeDtypeStruct((ROWS, 128), F32),
            in_specs=[vmem, vmem, smem, vmem],
            out_specs=vmem,
            scratch_shapes=[
                pltpu.VMEM((2, 128, 128), F32),
                pltpu.VMEM((R + 1, 128, 128), F32),
                pltpu.VMEM((R + 1, 2, 16), jnp.int32),
                pltpu.SMEM((R + 1, 2, 16), jnp.int32),
                pltpu.VMEM((2, TILES, 32, 128), F32),
                pltpu.VMEM((48, 32, 512), BF16),
                pltpu.VMEM((48, 16, TILE), F32),
                pltpu.VMEM((TILES * TILE, 32), BF16),
                pltpu.VMEM((TILE, 512), F32),
                pltpu.VMEM((TILE, 512), F32),
                pltpu.VMEM((TILE, 128), F32),
                pltpu.VMEM((TILE, 128), F32),
                pltpu.VMEM((TILE, 128), F32),
                pltpu.VMEM((TILE, 128), F32),
                pltpu.VMEM((R + 1, 40, 128), F32),
                pltpu.VMEM((R, ROWS, 128), F32),
                pltpu.VMEM((32 * (R + 1), TILE), F32),
                pltpu.VMEM((1, 128), jnp.int32),
                pltpu.VMEM((96, 128), F32),
                pltpu.VMEM((2, ROWS, 128), F32),
                dma((R,)),
                dma((R,)),
                dma((2,)),
                dma((2,)),
                dma((R,)),
                dma((R,)),
                dma((R,)),
                dma((R,)),
                dma((2,)),
                dma((2,)),
                dma((R + 1,)),
            ],
            compiler_params=pltpu.CompilerParams(collective_id=0, has_side_effects=True),
        )(
            coords.reshape(3 * ROWS, 128),
            masses.reshape(ROWS, 128),
            counts.reshape(TILES),
            jnp.transpose(lists.reshape(R + 1, TILES, 2), (0, 2, 1)),
        )
        return density.reshape(1, 1, -1)

    return jax.shard_map(
        on_device, mesh=mesh, in_specs=placed, out_specs=P("chan", "wall", None), check_vma=False
    )
```

time: 67.2 us -> 55.7 us (0.83)
  the two profiles are of different devices: /device:TPU:4 before, /device:TPU:7 now
where the time goes in v2:
time: 55.7 us; the launch traced here: 55.4 us
  Pallas kernels  54.1 us (97%)
  local copies, waits for them, and re-layouts  1.32 us (2%)
    pallas_call x1, Pallas kernels, on_device(): pl.pallas_call(functools.partial(kernel, chan_count, wall_count), out_sha...  54.1 us
    unnamed x1, local copies, waits for them, and re-layouts  1.32 us

profile of v2, /device:TPU:7, one launch (start us, length us, event | category | flops | bytes accessed | tf_op | source)
XLA Modules:
  0.0 55.4 jit_solution(6129335594662491240)
XLA Ops:
  0.0 54.1 %shard_map.46 = f32[32,128]{1,0:T(8,128)} custom-call(f32[96,128]{1,0:T(8,128)} %bitcast.8, f32[32,128]{1,0:T(8,128)} %bitcast.9, s32[16]{0:T(128)} %bitcast.11, s32[5,2,16]{2,1,0:T(2,128)} %bitcast.10), custom_call_target="tpu_custom_call" | custom-call | tf_op jit(solution)/shard_map/pallas_call | solution.py:469
  54.1 1.3 %copy.6 = f32[1,1,4096]{2,1,0:T(1,128)} copy(f32[1,1,4096]{2,1,0:T(1,128)} %bitcast.7) | data formatting | bytes 32768
